TPU v7x, 32 devices: a whole 2x2x4 slice. The times are simulated.
32 devices in a mesh: row: 8 (over y, x, core), col: 4 (over z).
Axes of the slice: x: 2, y: 2, z: 4, core: 2. Of those that a mesh axis runs over, the one named last changes fastest.
Arguments:
- features: bfloat16 [65536, 256], P(('row', 'col')), may hold values from -6 to 6
- tiles: bfloat16 [8, 4, 768, 128, 128], P('row', 'col'), as said below
- tile_rows: int32 [8, 4, 768], P('row', 'col'), may hold values from 0 to 63
- tile_cols: int32 [8, 4, 768], P('row', 'col'), may hold values from 0 to 127
- valid: int32 [8, 4, 768], P('row', 'col'), may hold values from 0 to 1, as said below
- weight: bfloat16 [256, 256], replicated, may hold values from -0.375 to 0.375
- bias: float32 [256], replicated, may hold values from -3 to 3
Outputs:
- hidden: bfloat16 [65536, 256], P(('row', 'col'))
Inputs may be any that keep to these rules, and one draw needn't show every extreme that they name: Each cell holds between 96 and 384 valid slots at any positions; in every draw some cell has exactly 384 valid slots. `tiles`: tile entries are non-negative.
All inputs are finite; a program needn't handle non-finite values.
Results may differ from a plain program's by a relative error of at most 0.0039.
Values may be sent and summed in bfloat16 or wider, within the bound.
A program may use at most 256 MiB of HBM per device.

v0:
```python
import functools

import jax
import jax.numpy as jnp
from jax import lax
from jax.experimental import pallas as pl
from jax.experimental.pallas import tpu as pltpu
from jax.sharding import PartitionSpec as P

SLOTS = 32
UNROLL = 8


def spmm_kernel(valid, rows, cols, panel_hbm, tiles_hbm, total,
                slot_list, row_list, col_list, panel, ring, ring_sem, panel_sem):
    slot_count = valid.shape[2]
    row_tiles = total.shape[0] - 1
    panel_copy = pltpu.make_async_copy(panel_hbm, panel, panel_sem)
    panel_copy.start()

    def scan(step, count):
        for k in range(UNROLL):
            slot = step * UNROLL + k
            slot_list[count] = slot
            row_list[count] = rows[0, 0, slot]
            col_list[count] = cols[0, 0, slot]
            count = count + valid[0, 0, slot]
        return count

    count = lax.fori_loop(0, slot_count // UNROLL, scan, jnp.int32(0))
    for k in range(UNROLL):
        slot_list[count + k] = 0
        row_list[count + k] = row_tiles
        col_list[count + k] = 0
    steps = (count + UNROLL - 1) // UNROLL
    filled = steps * UNROLL

    def fetch(index):
        place = lax.rem(index, SLOTS)
        return pltpu.make_async_copy(
            tiles_hbm.at[0, 0, slot_list[index]], ring.at[place], ring_sem.at[place])

    def prime(index, carry):
        @pl.when(index < filled)
        def _():
            fetch(index).start()
        return carry

    lax.fori_loop(0, SLOTS, prime, 0)
    total[...] = jnp.zeros_like(total)
    panel_copy.wait()

    def step_body(step, carry):
        base = step * UNROLL
        for k in range(UNROLL):
            fetch(base + k).wait()
        for k in range(UNROLL):
            index = base + k
            product = jnp.dot(ring[lax.rem(index, SLOTS)], panel[col_list[index]],
                              preferred_element_type=jnp.float32)
            row = row_list[index]
            total[row] = total[row] + product
        for k in range(UNROLL):
            later = base + SLOTS + k

            @pl.when(later < filled)
            def _():
                fetch(later).start()
        return carry

    lax.fori_loop(0, steps, step_body, 0)


def spmm(valid, rows, cols, panel, tiles, row_tiles):
    slot_count, tile_size = tiles.shape[2], tiles.shape[3]
    width = panel.shape[2]
    smem = pl.BlockSpec(memory_space=pltpu.SMEM)
    hbm = pl.BlockSpec(memory_space=pl.ANY)
    return pl.pallas_call(
        spmm_kernel,
        out_shape=jax.ShapeDtypeStruct((row_tiles + 1, tile_size, width), jnp.float32),
        in_specs=[smem, smem, smem, hbm, hbm],
        out_specs=pl.BlockSpec(memory_space=pltpu.VMEM),
        scratch_shapes=[
            pltpu.SMEM((slot_count + UNROLL,), jnp.int32),
            pltpu.SMEM((slot_count + UNROLL,), jnp.int32),
            pltpu.SMEM((slot_count + UNROLL,), jnp.int32),
            pltpu.VMEM(panel.shape, jnp.bfloat16),
            pltpu.VMEM((SLOTS, tile_size, tile_size), jnp.bfloat16),
            pltpu.SemaphoreType.DMA((SLOTS,)),
            pltpu.SemaphoreType.DMA,
        ],
        compiler_params=pltpu.CompilerParams(vmem_limit_bytes=60 * 2**20),
        cost_estimate=pl.CostEstimate(
            flops=slot_count * tile_size * tile_size * width, bytes_accessed=32 * 2**20,
            transcendentals=0),
    )(valid, rows, cols, panel, tiles)


MESH = pl.DeviceIdType.MESH
PIECES = 2


def gather_steps(features, lane, panel, send_sem, recv_sem, local_sem, rows):
    sub_rows, width = panel.shape[1], panel.shape[2]
    cut = sub_rows // 2
    me = lax.axis_index("row")
    chips = rows // 2
    core, chip = lax.rem(me, 2), me // 2
    partner = chip * 2 + (1 - core)
    own = features.at[:, pl.ds(lane * width, width)]

    def half(ref, k):
        return ref.at[pl.ds(k * cut, cut)]

    def copy(src, block, k, number, target):
        return pltpu.make_async_remote_copy(
            src_ref=src, dst_ref=half(panel.at[block], k), send_sem=send_sem.at[number],
            recv_sem=recv_sem.at[number], device_id={"row": target}, device_id_type=MESH)

    def held(block, k):
        return half(panel.at[block], k)

    if chips == 4:
        over_x, over_y = lax.rem(chip, 2), chip // 2
        x_side = (over_y * 2 + (1 - over_x)) * 2 + core
        y_side = ((1 - over_y) * 2 + over_x) * 2 + core
        across = ((1 - over_y) * 2 + (1 - over_x)) * 2 + core
        peers = [x_side, y_side]
        sources = [x_side, y_side, y_side, x_side]
        own_copies = [copy(half(own, 0), me, 0, 0, x_side), copy(half(own, 1), me, 1, 1, y_side),
                      copy(half(own, 1), me, 1, 2, x_side), copy(half(own, 0), me, 0, 3, y_side)]
        passed = {0: copy(held(x_side, 0), x_side, 0, 4, y_side),
                  1: copy(held(y_side, 1), y_side, 1, 5, x_side)}
        arriving = [(x_side, 0), (y_side, 1), (x_side, 1), (y_side, 0), (across, 0), (across, 1)]
    else:
        peers = [lax.rem(chip + k, chips) * 2 + core for k in range(1, chips)]
        from_peers = [lax.rem(chip + chips - k, chips) * 2 + core for k in range(1, chips)]
        own_copies, passed, arriving = [], {}, []
        for place, (peer, giver) in enumerate(zip(peers, from_peers)):
            for k in range(2):
                own_copies.append(copy(half(own, k), me, k, 2 * place + k, peer))
                arriving.append((giver, k))
    direct = len(arriving)
    started = list(own_copies)
    keep = pltpu.make_async_copy(own, panel.at[me], local_sem)

    def begin():
        for item in own_copies:
            item.start()
        for k in range(2):
            item = copy(half(own, k), me, k, direct + k, partner)
            item.start()
            started.append(item)
        keep.start()

    def receive(number):
        block, k = arriving[number]
        copy(held(block, k), block, k, number, partner).wait_recv()
        if number in passed:
            passed[number].start()
            started.append(passed[number])
        item = copy(held(block, k), block, k, direct + 2 + number, partner)
        item.start()
        started.append(item)

    def finish():
        for number in range(direct + 2):
            copy(held(me, 0), me, 0, direct + number, partner).wait_recv()
        for item in started:
            item.wait_send()
        keep.wait()

    steps = [functools.partial(receive, number) for number in range(direct)]
    return peers + [partner], begin, steps, finish


def reduce_steps(partial, summed, to_right, to_left, from_left, from_right, total, sems, columns):
    tiles_each = summed.shape[0]
    cut = tiles_each // PIECES
    me = lax.axis_index("col")
    right_send, right_recv, left_send, left_recv = sems

    def move(rightward, dest, piece):
        place = dest - 1 if rightward else dest
        outbox, inbox = (to_right, from_left) if rightward else (to_left, from_right)
        send, recv = (right_send, right_recv) if rightward else (left_send, left_recv)
        part = pl.ds(piece * cut, cut)
        inner = (me < dest) if rightward else (me > dest)
        first = (me == 0) if rightward else (me == columns - 1)
        number = place * PIECES + piece
        target = me + 1 if rightward else me - 1
        item = pltpu.make_async_remote_copy(
            src_ref=outbox.at[place, part], dst_ref=inbox.at[place, part],
            send_sem=send.at[number], recv_sem=recv.at[number],
            device_id={"col": target}, device_id_type=MESH)
        here = pl.ds(dest * tiles_each + piece * cut, cut)

        def open_chain():
            @pl.when(first)
            def _():
                outbox[place, part] = partial[here].astype(outbox.dtype)
                item.start()

        def pass_on():
            @pl.when(jnp.logical_and(inner, jnp.logical_not(first)))
            def _():
                item.wait_recv()
                outbox[place, part] = (
                    partial[here] + inbox[place, part].astype(jnp.float32)).astype(outbox.dtype)
                item.start()

        def close_chain():
            @pl.when(me == dest)
            def _():
                item.wait_recv()
                total[part] = total[part] + inbox[place, part].astype(jnp.float32)

        def drain():
            @pl.when(inner)
            def _():
                item.wait_send()

        return open_chain, pass_on, close_chain, drain

    links = []
    for turn in range(columns - 1):
        for piece in range(PIECES):
            links.append(move(True, columns - 1 - turn, piece))
            links.append(move(False, turn, piece))

    def begin():
        for link in links:
            link[0]()
        total[...] = partial[pl.ds(me * tiles_each, tiles_each)]

    def finish():
        for link in links:
            link[2]()
        summed[...] = total[...].astype(summed.dtype)
        for link in links:
            link[3]()

    return begin, [link[1] for link in links], finish


def exchange_kernel(gathering, reducing, lane, rows, columns, *refs):
    refs = list(refs)
    features = refs.pop(0) if gathering else None
    partial = refs.pop(0) if reducing else None
    panel = refs.pop(0) if gathering else None
    summed = refs.pop(0) if reducing else None
    peers, queue = [], []
    if gathering:
        send_sem, recv_sem, local_sem = refs.pop(0), refs.pop(0), refs.pop(0)
        peers, gather_begin, gather_list, gather_finish = gather_steps(
            features, lane, panel, send_sem, recv_sem, local_sem, rows)
    if reducing:
        reduce_begin, reduce_list, reduce_finish = reduce_steps(
            partial, summed, *refs[:5], refs[5:9], columns)

    barrier = pltpu.get_barrier_semaphore()
    for peer in peers:
        pl.semaphore_signal(barrier, inc=1, device_id={"row": peer}, device_id_type=MESH)
    expected = len(peers)
    if reducing:
        me = lax.axis_index("col")

        @pl.when(me > 0)
        def _():
            pl.semaphore_signal(barrier, inc=1, device_id={"col": me - 1}, device_id_type=MESH)

        @pl.when(me < columns - 1)
        def _():
            pl.semaphore_signal(barrier, inc=1, device_id={"col": me + 1}, device_id_type=MESH)

        inside = jnp.logical_and(me > 0, me < columns - 1)

        @pl.when(inside)
        def _():
            pl.semaphore_wait(barrier, expected + 2)

        @pl.when(jnp.logical_not(inside))
        def _():
            pl.semaphore_wait(barrier, expected + 1)
    else:
        pl.semaphore_wait(barrier, expected)

    if gathering:
        gather_begin()
    if reducing:
        reduce_begin()
    gather_queue = list(gather_list) if gathering else []
    reduce_queue = list(reduce_list) if reducing else []
    while gather_queue or reduce_queue:
        for queue in (gather_queue, reduce_queue):
            for _ in range(2):
                if queue:
                    queue.pop(0)()
    if gathering:
        gather_finish()
    if reducing:
        reduce_finish()


def exchange(number, features, lane, partial, width, tile_size, rows, columns):
    gathering, reducing = features is not None, partial is not None
    hbm, vmem = pl.BlockSpec(memory_space=pl.ANY), pl.BlockSpec(memory_space=pltpu.VMEM)
    operands, in_specs, out_shape, out_specs, scratch = [], [], [], [], []
    if gathering:
        sub_rows = features.shape[0]
        operands.append(features)
        in_specs.append(hbm)
        out_shape.append(jax.ShapeDtypeStruct((rows, sub_rows, width), jnp.bfloat16))
        out_specs.append(hbm)
        chips = rows // 2
        copies = 2 * (6 if chips == 4 else 2 * (chips - 1)) + 2
        scratch += [pltpu.SemaphoreType.DMA((copies,)), pltpu.SemaphoreType.DMA((copies,)),
                    pltpu.SemaphoreType.DMA]
    if reducing:
        tiles_each = (partial.shape[0] - 1) // columns
        operands.append(partial)
        in_specs.append(vmem)
        out_shape.append(jax.ShapeDtypeStruct((tiles_each, tile_size, width), jnp.bfloat16))
        out_specs.append(vmem)
        scratch += [pltpu.VMEM((columns - 1, tiles_each, tile_size, width), jnp.bfloat16)] * 4
        scratch += [pltpu.VMEM((tiles_each, tile_size, width), jnp.float32)]
        scratch += [pltpu.SemaphoreType.DMA(((columns - 1) * PIECES,))] * 4
    return pl.pallas_call(
        functools.partial(exchange_kernel, gathering, reducing, lane, rows, columns),
        out_shape=out_shape, in_specs=in_specs, out_specs=out_specs, scratch_shapes=scratch,
        compiler_params=pltpu.CompilerParams(
            collective_id=number, has_side_effects=True, vmem_limit_bytes=60 * 2**20),
    )(*operands)


def on_device(features, tiles, tile_rows, tile_cols, valid, weight, bias):
    sub_rows, channels = features.shape
    tile_size = tiles.shape[3]
    rows, columns = lax.axis_size("row"), lax.axis_size("col")
    row_tiles = sub_rows * columns // tile_size
    width = min(channels, 128)
    lanes = channels // width
    cells = (valid, tile_rows, tile_cols)
    sums, partial = [], None
    for lane in range(lanes + 1):
        results = list(exchange(
            lane, features if lane < lanes else None, lane, partial, width, tile_size, rows, columns))
        if partial is not None:
            sums.append(results.pop().reshape(sub_rows, width))
        if lane < lanes:
            panel = results[0].reshape(-1, tile_size, width)
            partial = spmm(*cells, panel, tiles, row_tiles)
    mixed = bias
    for lane in range(lanes):
        mixed = mixed + jnp.dot(sums[lane], weight[lane * width:(lane + 1) * width],
                                preferred_element_type=jnp.float32)
    return jnp.maximum(mixed, 0.0).astype(jnp.bfloat16)


def solution(mesh):
    return jax.shard_map(
        on_device,
        mesh=mesh,
        in_specs=(
            P(("row", "col"), None),
            P("row", "col", None, None, None),
            P("row", "col", None),
            P("row", "col", None),
            P("row", "col", None),
            P(),
            P(),
        ),
        out_specs=P(("row", "col"), None),
        check_vma=False,
    )
```

profile of v0, /device:TPU:18, one launch (start us, length us, event | category | flops | bytes accessed | tf_op | source)
XLA Modules:
  0.0 157.7 jit_solution(11556524302493960632)
XLA Ops:
  0.0 22.2 %shard_map.73 = bf16[8,2048,128]{2,1,0:T(8,128)(2,1)} custom-call(bf16[2048,256]{1,0:T(8,128)(2,1)} %refs_0_.3), custom_call_target="tpu_custom_call" | custom-call | tf_op jit(solution)/shard_map/pallas_call | solution.py:329
  22.2 19.6 %shard_map.74.refs_1_ = f32[65,128,128]{2,1,0:T(8,128)} custom-call(s32[1,1,768]{2,1,0:T(1,128)} %valid.3, s32[1,1,768]{2,1,0:T(1,128)} %rows.3, s32[1,1,768]{2,1,0:T(1,128)} %cols.3, bf16[128,128,128]{2,1,0:T(8,128)(2,1)} %bitcast.6, bf16[1,1,768,128,128]{4,3,2,1,0:T(8,128)(2,1)} %tiles_hbm.3), custom_call_target="tpu_custom_call" | custom-call | flops 1610612736 | bytes 33554432 | tf_op jit(solution)/shard_map/pallas_call | solution.py:79
  41.8 48.0 %shard_map.75 = (bf16[8,2048,128]{2,1,0:T(8,128)(2,1)}, bf16[16,128,128]{2,1,0:T(8,128)(2,1)}) custom-call(bf16[2048,256]{1,0:T(8,128)(2,1)} %refs_0_.3, f32[65,128,128]{2,1,0:T(8,128)} %shard_map.74.refs_1_), custom_call_target="tpu_custom_call" | custom-call | tf_op jit(solution)/shard_map/pallas_call | solution.py:329
  89.7 19.5 %shard_map.76.refs_0_ = f32[65,128,128]{2,1,0:T(8,128)} custom-call(s32[1,1,768]{2,1,0:T(1,128)} %valid.3, s32[1,1,768]{2,1,0:T(1,128)} %rows.3, s32[1,1,768]{2,1,0:T(1,128)} %cols.3, bf16[128,128,128]{2,1,0:T(8,128)(2,1)} %bitcast.7, bf16[1,1,768,128,128]{4,3,2,1,0:T(8,128)(2,1)} %tiles_hbm.3), custom_call_target="tpu_custom_call" | custom-call | flops 1610612736 | bytes 33554432 | tf_op jit(solution)/shard_map/pallas_call | solution.py:79
  109.3 0.0 copy-start.1
  109.3 0.0 copy-start.2
  109.3 0.0 copy-start.3
  109.3 46.0 %shard_map.77 = bf16[16,128,128]{2,1,0:T(8,128)(2,1)} custom-call(f32[65,128,128]{2,1,0:T(8,128)} %shard_map.76.refs_0_), custom_call_target="tpu_custom_call" | custom-call | tf_op jit(solution)/shard_map/pallas_call | solution.py:329
  155.3 0.0 copy-start
  155.3 0.0 copy-done.1
  155.3 0.0 copy-done.2
  155.3 0.0 copy-done.3
  155.3 0.4 convolution_add_fusion.1
  155.7 0.6 copy-done
  156.3 1.4 fusion.1
Async XLA Ops:
  109.3 46.0 %copy-start.1 = (bf16[16,128,128]{2,1,0:T(8,128)(2,1)S(1)}, bf16[16,128,128]{2,1,0:T(8,128)(2,1)}, u32[]{:S(2)}) copy-start(bf16[16,128,128]{2,1,0:T(8,128)(2,1)} %get-tuple-element.7) | copy-start | bytes 1572868
  109.3 46.0 %copy-start.2 = (bf16[256,256]{1,0:T(8,128)(2,1)S(1)}, bf16[256,256]{1,0:T(8,128)(2,1)}, u32[]{:S(2)}) copy-start(bf16[256,256]{1,0:T(8,128)(2,1)} %param.12) | copy-start | bytes 393220
  109.3 46.0 %copy-start.3 = (f32[256]{0:T(256)S(1)}, f32[256]{0:T(256)}, u32[]{:S(2)}) copy-start(f32[256]{0:T(256)} %param.13) | copy-start | bytes 3076
  155.3 1.0 copy-start
where the time goes:
time: 161 us; the launch traced here: 158 us
  Pallas kernels  155 us (96%)
  matrix products  1.8 us (1%)
    pallas_call x3, Pallas kernels, exchange(): pl.pallas_call(functools.partial(exchange_kernel, gathering, reducing, la...  116 us
    pallas_call x2, Pallas kernels, spmm(): pl.pallas_call(spmm_kernel, out_shape=jax.ShapeDtypeStruct((row_tiles + 1...  39.1 us

commit v1 on v0

--- a/solution.py
+++ b/solution.py
@@ -334,10 +334,420 @@
     )(*operands)
 
 
+LANES = 128
+FIELD_BITS = 10
+FIELD = 2**FIELD_BITS
+FIRST = FIELD * FIELD
+PAIR_UNROLL = 16
+CUTS = 4
+TILE_COPIES = 8
+VMEM_ROOM = 63 * 2**20
+
+
+def wanted_order(rows_v, cols_v, valid_v, codes_v, lasts_v, pairs):
+    slot_count = rows_v.shape[2]
+    lane = lax.broadcasted_iota(jnp.int32, (1, LANES), 1)
+    tall = lax.broadcasted_iota(jnp.int32, (LANES, LANES), 0)
+    tall_slots = lax.broadcasted_iota(jnp.int32, (slot_count, LANES), 0)
+    chunks = slot_count // LANES
+
+    def upright(pieces):
+        turned = [jnp.broadcast_to(piece, (LANES, LANES)).T for piece in pieces]
+        return turned[0] if len(turned) == 1 else jnp.concatenate(turned, axis=0)
+
+    def tally(hits, amounts):
+        return jnp.sum(jnp.where(hits, amounts, 0), axis=0, keepdims=True)
+
+    keys, columns_of = [], []
+    for chunk in range(chunks):
+        part = pl.ds(chunk * LANES, LANES)
+        keys.append(jnp.where(valid_v[0, :, part] > 0, rows_v[0, :, part], -1))
+        columns_of.append(cols_v[0, :, part])
+    key_tall = upright(keys)
+    held = tally(key_tall == lane, 1)
+    halves = lax.shift_right_logical(held + 1, 1)
+    halves_tall = upright([halves])
+    lasts_v[...] = jnp.where(
+        held > 0, tally(tall < lane, halves_tall) + halves - 1, pairs)
+    places, codes = [], []
+    for chunk in range(chunks):
+        slot = lane + chunk * LANES
+        before = tally(jnp.logical_and(key_tall == keys[chunk], tall_slots < slot), 1)
+        start = tally(tall < keys[chunk], halves_tall)
+        places.append(jnp.where(keys[chunk] >= 0, 2 * start + before, -1))
+        codes.append(slot - slot_count + columns_of[chunk] * FIELD
+                     + jnp.where(before == 0, FIRST, 0))
+    place_tall, code_tall = upright(places), upright(codes)
+    for chunk in range(codes_v.shape[1] // LANES):
+        found = tally(place_tall == lane + chunk * LANES, code_tall)
+        codes_v[:, pl.ds(chunk * LANES, LANES)] = found + slot_count
+
+
+def multiply(codes, tiles, panel, prefix, pairs):
+    def operands(code):
+        column = jnp.bitwise_and(lax.shift_right_logical(code, FIELD_BITS), FIELD - 1)
+        return tiles[jnp.bitwise_and(code, FIELD - 1)], panel[column]
+
+    def body(step, total):
+        for k in range(PAIR_UNROLL):
+            pair = step * PAIR_UNROLL + k
+            code = codes[0, 2 * pair]
+            left, upper = operands(code)
+            right, lower = operands(codes[0, 2 * pair + 1])
+            product = jnp.dot(jnp.concatenate([left, right], axis=1),
+                              jnp.concatenate([upper, lower], axis=0),
+                              preferred_element_type=jnp.float32)
+            opens = jnp.full(total.shape, code, jnp.int32) >= FIRST
+            total = jnp.where(opens, 0.0, total) + product
+            prefix[pair] = total
+        return total
+
+    lax.fori_loop(0, pairs // PAIR_UNROLL, body, jnp.zeros(panel.shape[1:], jnp.float32))
+
+
+def gather_lane(panel, send_sem, recv_sem, sub_tiles):
+    cut = sub_tiles // 2
+    me = lax.axis_index("row")
+    core, chip = lax.rem(me, 2), me // 2
+    partner = chip * 2 + (1 - core)
+    over_x, over_y = lax.rem(chip, 2), chip // 2
+    x_side = (over_y * 2 + (1 - over_x)) * 2 + core
+    y_side = ((1 - over_y) * 2 + over_x) * 2 + core
+    across = ((1 - over_y) * 2 + (1 - over_x)) * 2 + core
+
+    def copy(block, k, number, target):
+        part = panel.at[pl.ds(block * sub_tiles + k * cut, cut)]
+        return pltpu.make_async_remote_copy(
+            src_ref=part, dst_ref=part, send_sem=send_sem.at[number],
+            recv_sem=recv_sem.at[number], device_id={"row": target}, device_id_type=MESH)
+
+    own = [copy(me, 0, 0, x_side), copy(me, 1, 1, y_side),
+           copy(me, 1, 2, x_side), copy(me, 0, 3, y_side)]
+    passed = {0: copy(x_side, 0, 4, y_side), 1: copy(y_side, 1, 5, x_side)}
+    arriving = [(x_side, 0), (y_side, 1), (x_side, 1), (y_side, 0), (across, 0), (across, 1)]
+    direct = len(arriving)
+    started = []
+
+    def start(item):
+        item.start()
+        started.append(item)
+
+    def begin():
+        for item in own:
+            start(item)
+        for k in range(2):
+            start(copy(me, k, direct + k, partner))
+
+    def receive(number):
+        block, k = arriving[number]
+        copy(block, k, number, partner).wait_recv()
+        if number in passed:
+            start(passed[number])
+        start(copy(block, k, direct + 2 + number, partner))
+
+    def finish():
+        for number in range(direct + 2):
+            copy(me, 0, direct + number, partner).wait_recv()
+
+    def drain():
+        for item in started:
+            item.wait_send()
+
+    return [x_side, y_side, partner], begin, receive, finish, drain
+
+
+def reduce_lane(prefix, lasts, partial, boxes, sems, columns):
+    tiles_each = boxes.shape[1]
+    cut = tiles_each // CUTS
+    me = lax.axis_index("col")
+    ends = jnp.logical_or(me == 0, me == columns - 1)
+    send, recv = sems
+
+    def link(rightward, dest, piece):
+        part = pl.ds(piece * cut, cut)
+        place = dest - 1 if rightward else dest
+        number = ((0 if rightward else 1) * (columns - 1) + place) * CUTS + piece
+        target = me + 1 if rightward else me - 1
+        here = dest - me if rightward else columns - me + dest
+        there = here - 1 if rightward else here + 1
+        inner = (me < dest) if rightward else (me > dest)
+        first = (me == 0) if rightward else (me == columns - 1)
+
+        def outgoing():
+            return pltpu.make_async_remote_copy(
+                src_ref=boxes.at[here, part], dst_ref=boxes.at[there, part],
+                send_sem=send.at[number], recv_sem=recv.at[number],
+                device_id={"col": target}, device_id_type=MESH)
+
+        def incoming():
+            return pltpu.make_async_remote_copy(
+                src_ref=boxes.at[here, part], dst_ref=boxes.at[here, part],
+                send_sem=send.at[number], recv_sem=recv.at[number],
+                device_id={"col": target}, device_id_type=MESH)
+
+        def open_chain():
+            @pl.when(first)
+            def _():
+                def body(k, carry):
+                    tile = piece * cut + k
+                    boxes[here, tile] = prefix[lasts[0, dest * tiles_each + tile]].astype(boxes.dtype)
+                    return carry
+                lax.fori_loop(0, cut, body, 0)
+                outgoing().start()
+
+        def pass_on():
+            @pl.when(jnp.logical_and(inner, jnp.logical_not(first)))
+            def _():
+                incoming().wait_recv()
+
+                def body(k, carry):
+                    tile = piece * cut + k
+                    boxes[here, tile] = (
+                        partial[dest * tiles_each + tile]
+                        + boxes[here, tile].astype(jnp.float32)).astype(boxes.dtype)
+                    return carry
+                lax.fori_loop(0, cut, body, 0)
+                outgoing().start()
+
+        def close_chain():
+            @pl.when(jnp.logical_and(me == dest, jnp.logical_not(first)))
+            def _():
+                incoming().wait_recv()
+
+                def body(k, carry):
+                    tile = piece * cut + k
+                    own = dest * tiles_each + tile
+                    partial[own] = partial[own] + boxes[here, tile].astype(jnp.float32)
+                    return carry
+                lax.fori_loop(0, cut, body, 0)
+
+        def drain():
+            @pl.when(inner)
+            def _():
+                outgoing().wait_send()
+
+        return open_chain, pass_on, close_chain, drain
+
+    links = []
+    for turn in range(columns - 1):
+        for piece in range(CUTS):
+            links.append(link(True, columns - 1 - turn, piece))
+            links.append(link(False, turn, piece))
+
+    def begin():
+        for item in links:
+            item[0]()
+
+        @pl.when(jnp.logical_not(ends))
+        def _():
+            def body(tile, carry):
+                partial[tile] = prefix[lasts[0, tile]]
+                return carry
+            lax.fori_loop(0, columns * tiles_each, body, 0)
+
+        @pl.when(ends)
+        def _():
+            def body(k, carry):
+                tile = me * tiles_each + k
+                partial[tile] = prefix[lasts[0, tile]]
+                return carry
+            lax.fori_loop(0, tiles_each, body, 0)
+
+    passes = [item[1] for item in links]
+
+    def close(piece):
+        for dest in range(columns):
+            if dest > 0:
+                link(True, dest, piece)[2]()
+            if dest < columns - 1:
+                link(False, dest, piece)[2]()
+
+    def drain():
+        for item in links:
+            item[3]()
+
+    return begin, passes, close, drain
+
+
+def layer_kernel(rows, columns, pairs, features, tiles_hbm, tile_rows, tile_cols, valid, weight_hbm,
+                 bias_hbm, out, tiles, prefix, rows_v, cols_v, valid_v, codes_v, lasts_v, codes,
+                 lasts, weight, bias, result, panels, partials, boxes, gather_sems, reduce_sems,
+                 local_sems, tile_sems, out_sems):
+    sub_tiles = features.shape[0]
+    tile_size, width = panels[0].shape[1:]
+    slot_count = tiles_hbm.shape[2]
+    lanes = len(panels)
+    me_row, me_col = lax.axis_index("row"), lax.axis_index("col")
+
+    def local(number, src, dst):
+        return pltpu.make_async_copy(src, dst, local_sems.at[number])
+
+    owns = []
+    for lane in range(lanes):
+        owns.append(local(lane, features.at[:, :, pl.ds(lane * width, width)],
+                          panels[lane].at[pl.ds(me_row * sub_tiles, sub_tiles)]))
+    small = [local(lanes, tile_rows, rows_v), local(lanes + 1, tile_cols, cols_v),
+             local(lanes + 2, valid, valid_v)]
+    params = [local(lanes + 3, weight_hbm, weight), local(lanes + 4, bias_hbm, bias)]
+    share = slot_count // TILE_COPIES
+    loads = []
+    for k in range(TILE_COPIES):
+        part = pl.ds(k * share, share)
+        loads.append(pltpu.make_async_copy(
+            tiles_hbm.at[0, 0, part], tiles.at[part], tile_sems.at[k]))
+    for item in owns + small + params + loads:
+        item.start()
+
+    gathers = [gather_lane(panels[lane], *gather_sems[lane], sub_tiles) for lane in range(lanes)]
+    reduces = [reduce_lane(prefix, lasts, partials[lane], boxes[lane], reduce_sems[lane], columns)
+               for lane in range(lanes)]
+
+    barrier = pltpu.get_barrier_semaphore()
+    peers = gathers[0][0]
+    for peer in peers:
+        pl.semaphore_signal(barrier, inc=1, device_id={"row": peer}, device_id_type=MESH)
+
+    @pl.when(me_col > 0)
+    def _():
+        pl.semaphore_signal(barrier, inc=1, device_id={"col": me_col - 1}, device_id_type=MESH)
+
+    @pl.when(me_col < columns - 1)
+    def _():
+        pl.semaphore_signal(barrier, inc=1, device_id={"col": me_col + 1}, device_id_type=MESH)
+
+    inside = jnp.logical_and(me_col > 0, me_col < columns - 1)
+
+    @pl.when(inside)
+    def _():
+        pl.semaphore_wait(barrier, len(peers) + 2)
+
+    @pl.when(jnp.logical_not(inside))
+    def _():
+        pl.semaphore_wait(barrier, len(peers) + 1)
+
+    owns[0].wait()
+    gathers[0][1]()
+    for item in small:
+        item.wait()
+    wanted_order(rows_v, cols_v, valid_v, codes_v, lasts_v, pairs)
+    lists = [local(lanes, codes_v, codes), local(lanes + 1, lasts_v, lasts)]
+    for item in lists:
+        item.start()
+    tiles[slot_count] = jnp.zeros(tiles.shape[1:], tiles.dtype)
+    prefix[pairs] = jnp.zeros(prefix.shape[1:], prefix.dtype)
+
+    for lane in range(lanes):
+        _, _, receive, finish, _ = gathers[lane]
+        early = list(reduces[lane - 1][1]) if lane > 0 else []
+        for number in range(2):
+            receive(number)
+        if lane + 1 < lanes:
+            owns[lane + 1].wait()
+            gathers[lane + 1][1]()
+        for number in range(2, 6):
+            if number % 2 == 0:
+                for _ in range(CUTS):
+                    if early:
+                        early.pop(0)()
+            receive(number)
+        finish()
+        if lane == 0:
+            for item in lists + loads:
+                item.wait()
+        multiply(codes, tiles, panels[lane], prefix, pairs)
+        reduces[lane][0]()
+        for item in early:
+            item()
+    for item in reduces[-1][1]:
+        item()
+    for item in params:
+        item.wait()
+    tiles_each = boxes[0].shape[1]
+    cut = tiles_each // CUTS
+    outs = []
+    for piece in range(CUTS):
+        for lane in range(lanes):
+            reduces[lane][2](piece)
+
+        def body(k, carry):
+            tile = piece * cut + k
+            summed = jnp.concatenate(
+                [partial[me_col * tiles_each + tile].astype(jnp.bfloat16) for partial in partials],
+                axis=1)
+            mixed = jnp.dot(summed, weight[...], preferred_element_type=jnp.float32) + bias[...]
+            start = pl.multiple_of(tile * tile_size, tile_size)
+            result[pl.ds(start, tile_size), :] = jnp.maximum(mixed, 0.0).astype(result.dtype)
+            return carry
+
+        lax.fori_loop(0, cut, body, 0)
+        part = pl.ds(piece * cut * tile_size, cut * tile_size)
+        item = pltpu.make_async_copy(result.at[part], out.at[part], out_sems.at[piece])
+        item.start()
+        outs.append(item)
+    for lane in range(lanes):
+        gathers[lane][4]()
+        reduces[lane][3]()
+    for item in outs:
+        item.wait()
+
+
+def layer(features, tiles, tile_rows, tile_cols, valid, weight, bias, rows, columns):
+    sub_rows, channels = features.shape
+    slot_count, tile_size = tiles.shape[2], tiles.shape[3]
+    lanes = channels // LANES
+    row_tiles = sub_rows * columns // tile_size
+    pairs = -(-(slot_count // 2 + row_tiles) // (2 * PAIR_UNROLL)) * PAIR_UNROLL
+    tiles_each = row_tiles // columns
+    codes_room = -(-2 * pairs // LANES) * LANES
+    vmem, smem, dma = pltpu.VMEM, pltpu.SMEM, pltpu.SemaphoreType.DMA
+    copies, moves = 14, 2 * (columns - 1) * CUTS
+    scratch = [
+        vmem((slot_count + 1, tile_size, tile_size), jnp.bfloat16),
+        vmem((pairs + 1, tile_size, LANES), jnp.float32),
+        vmem(tile_rows.shape, jnp.int32), vmem(tile_cols.shape, jnp.int32), vmem(valid.shape, jnp.int32),
+        vmem((1, codes_room), jnp.int32), vmem((1, LANES), jnp.int32),
+        smem((1, codes_room), jnp.int32), smem((1, LANES), jnp.int32),
+        vmem(weight.shape, weight.dtype), vmem((1, channels), bias.dtype),
+        vmem(features.shape, jnp.bfloat16),
+        [vmem((rows * tiles_each, tile_size, LANES), jnp.bfloat16)] * lanes,
+        [vmem((row_tiles, tile_size, LANES), jnp.float32)] * lanes,
+        [vmem((columns + 1, tiles_each, tile_size, LANES), jnp.bfloat16)] * lanes,
+        [[dma((copies,))] * 2] * lanes,
+        [[dma((moves,))] * 2] * lanes,
+        dma((lanes + 5,)), dma((TILE_COPIES,)), dma((CUTS,)),
+    ]
+    hbm = pl.BlockSpec(memory_space=pl.ANY)
+    return pl.pallas_call(
+        functools.partial(layer_kernel, rows, columns, pairs),
+        out_shape=jax.ShapeDtypeStruct(features.shape, jnp.bfloat16),
+        in_specs=[hbm] * 7, out_specs=hbm, scratch_shapes=scratch,
+        compiler_params=pltpu.CompilerParams(
+            collective_id=0, has_side_effects=True, vmem_limit_bytes=VMEM_ROOM),
+    )(features.reshape(tiles_each, tile_size, channels), tiles, tile_rows, tile_cols, valid, weight,
+      bias.reshape(1, channels))
+
+
+def fits(features, tiles, rows, columns):
+    sub_rows, channels = features.shape
+    slot_count, tile_size = tiles.shape[2], tiles.shape[3]
+    if rows != 8 or channels % LANES or tile_size != LANES or slot_count % LANES or slot_count >= FIELD:
+        return False
+    row_tiles = sub_rows * columns // tile_size
+    col_tiles = sub_rows * rows // tile_size
+    tile_bytes = tile_size * tile_size * 2
+    lanes = channels // LANES
+    pairs = (slot_count // 2 + row_tiles) // 2 + PAIR_UNROLL
+    held = slot_count + 2 * pairs + lanes * (
+        col_tiles + 2 * row_tiles + (columns + 1) * row_tiles // columns)
+    return row_tiles <= LANES and held * tile_bytes < VMEM_ROOM - 2 * 2**20
+
+
 def on_device(features, tiles, tile_rows, tile_cols, valid, weight, bias):
     sub_rows, channels = features.shape
     tile_size = tiles.shape[3]
     rows, columns = lax.axis_size("row"), lax.axis_size("col")
+    if fits(features, tiles, rows, columns):
+        return layer(features, tiles, tile_rows, tile_cols, valid, weight, bias, rows, columns)
     row_tiles = sub_rows * columns // tile_size
     width = min(channels, 128)
     lanes = channels // width

time: 161 us -> 137 us (0.85); the launches traced: 158 us -> 137 us
  Pallas kernels: 155 us -> 134 us
  matrix products: 1.8 us -> 0 us
  local copies, waits for them, and re-layouts: 0.6 us -> 2.26 us
    pallas_call x5 -> x1, Pallas kernels: 155 us -> 134 us  [layer(): pl.pallas_call(functools.partial(layer_kernel, rows, columns, pairs), out...]
    dot_general x2 -> x0, matrix products: 1.8 us -> none  [on_device(): jnp.dot(sums[lane], weight[lane * width:(lane + 1) * width], preferred_el...]
    unnamed x8 -> x1, local copies, waits for them, and re-layouts: 0.6 us -> 2.26 us
where the time goes in v1:
time: 137 us
  Pallas kernels  134 us (98%)
  local copies, waits for them, and re-layouts  2.26 us (2%)
    pallas_call x1, Pallas kernels, layer(): pl.pallas_call(functools.partial(layer_kernel, rows, columns, pairs), out...  134 us

profile of v1, /device:TPU:18, one launch (start us, length us, event | category | flops | bytes accessed | tf_op | source)
XLA Modules:
  0.0 136.6 jit_solution(8197873933544552790)
XLA Ops:
  0.0 134.3 %shard_map.73 = bf16[2048,256]{1,0:T(8,128)(2,1)} custom-call(bf16[16,128,256]{2,1,0:T(8,128)(2,1)} %bitcast.2, bf16[1,1,768,128,128]{4,3,2,1,0:T(8,128)(2,1)} %tiles_hbm.1, s32[1,1,768]{2,1,0:T(1,128)} %tile_rows.1, s32[1,1,768]{2,1,0:T(1,128)} %tile_cols.1, s32[1,1,768]{2,1,0:T(1,128)} %valid.1, bf16[256,256]{1,0:T(8,128)(2,1)} %weight_hbm.1, f32[1,256]{1,0:T(1,128)} %bitcast.3), custom_call_target="tpu_custom_call" | custom-call | tf_op jit(solution)/shard_map/pallas_call | solution.py:720
  134.3 2.3 %copy.9 = bf16[2048,256]{1,0:T(8,128)(2,1)} copy(bf16[2048,256]{1,0:T(8,128)(2,1)} %shard_map.73) | data formatting | bytes 2097152

commit v2 on v0

--- a/solution.py
+++ b/solution.py
@@ -334,10 +334,514 @@
     )(*operands)
 
 
+LANES = 128
+FIELD_BITS = 10
+FIELD = 2**FIELD_BITS
+FIRST = FIELD * FIELD
+PAIR_UNROLL = 16
+CUTS = 4
+TILE_COPIES = 8
+VMEM_ROOM = 63 * 2**20
+TILE_TIME, HOP_TIME, PRODUCT_TIME, ENTRY_TIME = 0.7, 1.8, 6.0, 3.0
+
+
+def group_widths(channels):
+    half = LANES // 2
+    return (half, half) + (LANES,) * ((channels - LANES) // LANES)
+
+
+def wanted_order(rows_v, cols_v, valid_v, codes_v, lasts_v, pairs):
+    slot_count = rows_v.shape[2]
+    lane = lax.broadcasted_iota(jnp.int32, (1, LANES), 1)
+    tall = lax.broadcasted_iota(jnp.int32, (LANES, LANES), 0)
+    tall_slots = lax.broadcasted_iota(jnp.int32, (slot_count, LANES), 0)
+    chunks = slot_count // LANES
+
+    def upright(pieces):
+        turned = [jnp.broadcast_to(piece, (LANES, LANES)).T for piece in pieces]
+        return turned[0] if len(turned) == 1 else jnp.concatenate(turned, axis=0)
+
+    def tally(hits, amounts):
+        return jnp.sum(jnp.where(hits, amounts, 0), axis=0, keepdims=True)
+
+    keys, columns_of = [], []
+    for chunk in range(chunks):
+        part = pl.ds(chunk * LANES, LANES)
+        keys.append(jnp.where(valid_v[0, :, part] > 0, rows_v[0, :, part], -1))
+        columns_of.append(cols_v[0, :, part])
+    key_tall = upright(keys)
+    held = tally(key_tall == lane, 1)
+    halves = lax.shift_right_logical(held + 1, 1)
+    halves_tall = upright([halves])
+    lasts_v[...] = jnp.where(
+        held > 0, tally(tall < lane, halves_tall) + halves - 1, pairs)
+    places, codes = [], []
+    for chunk in range(chunks):
+        slot = lane + chunk * LANES
+        before = tally(jnp.logical_and(key_tall == keys[chunk], tall_slots < slot), 1)
+        start = tally(tall < keys[chunk], halves_tall)
+        places.append(jnp.where(keys[chunk] >= 0, 2 * start + before, -1))
+        codes.append(slot - slot_count + columns_of[chunk] * FIELD
+                     + jnp.where(before == 0, FIRST, 0))
+    place_tall, code_tall = upright(places), upright(codes)
+    for chunk in range(codes_v.shape[1] // LANES):
+        found = tally(place_tall == lane + chunk * LANES, code_tall)
+        codes_v[:, pl.ds(chunk * LANES, LANES)] = found + slot_count
+
+
+def pack_own(own, panel, place, sub_tiles, width, channel):
+    packed = LANES // width
+    each = sub_tiles // packed
+    lane = lax.broadcasted_iota(jnp.int32, own.shape[1:2] + (LANES,), 1)
+    chunk, offset = channel // LANES, channel % LANES
+
+    def body(k, carry):
+        value = None
+        for h in range(packed):
+            piece = own[h * each + k, :, pl.ds(chunk * LANES, LANES)].astype(jnp.float32)
+            turn = (h * width - offset) % LANES
+            piece = pltpu.roll(piece, turn, 1) if turn else piece
+            value = piece if value is None else jnp.where(lane >= h * width, piece, value)
+        panel[place + k] = value.astype(panel.dtype)
+        return carry
+
+    lax.fori_loop(0, each, body, 0)
+
+
+def multiply(codes, tiles, panel, prefix, masks, pairs, sub_tiles):
+    packed = masks.shape[0] if masks is not None else 1
+    each = sub_tiles // packed
+
+    def operands(code):
+        column = jnp.bitwise_and(lax.shift_right_logical(code, FIELD_BITS), FIELD - 1)
+        tile = tiles[jnp.bitwise_and(code, FIELD - 1)]
+        if packed == 1:
+            return tile, panel[column]
+        bits = each.bit_length() - 1
+        upper = lax.shift_right_logical(column, bits)
+        block = lax.shift_right_logical(upper, packed.bit_length() - 1)
+        share = jnp.bitwise_and(upper, packed - 1)
+        value = panel[block * each + jnp.bitwise_and(column, each - 1)]
+        return tile, value * masks[share]
+
+    def body(step, total):
+        for k in range(PAIR_UNROLL):
+            pair = step * PAIR_UNROLL + k
+            code = codes[0, 2 * pair]
+            left, upper = operands(code)
+            right, lower = operands(codes[0, 2 * pair + 1])
+            product = jnp.dot(jnp.concatenate([left, right], axis=1),
+                              jnp.concatenate([upper, lower], axis=0),
+                              preferred_element_type=jnp.float32)
+            opens = jnp.full(total.shape, code, jnp.int32) >= FIRST
+            total = jnp.where(opens, 0.0, total) + product
+            prefix[pair] = total
+        return total
+
+    lax.fori_loop(0, pairs // PAIR_UNROLL, body, jnp.zeros(panel.shape[1:], jnp.float32))
+
+
+def gather_group(panel, send_sem, recv_sem, each):
+    cut = each // 2
+    me = lax.axis_index("row")
+    core, chip = lax.rem(me, 2), me // 2
+    partner = chip * 2 + (1 - core)
+    over_x, over_y = lax.rem(chip, 2), chip // 2
+    x_side = (over_y * 2 + (1 - over_x)) * 2 + core
+    y_side = ((1 - over_y) * 2 + over_x) * 2 + core
+    across = ((1 - over_y) * 2 + (1 - over_x)) * 2 + core
+
+    def copy(block, k, number, target):
+        part = panel.at[pl.ds(block * each + k * cut, cut)]
+        return pltpu.make_async_remote_copy(
+            src_ref=part, dst_ref=part, send_sem=send_sem.at[number],
+            recv_sem=recv_sem.at[number], device_id={"row": target}, device_id_type=MESH)
+
+    own = [(me, 0, 0, x_side), (me, 1, 1, y_side), (me, 1, 2, x_side), (me, 0, 3, y_side)]
+    passed = {0: (x_side, 0, 4, y_side), 1: (y_side, 1, 5, x_side)}
+    arriving = [(x_side, 0), (y_side, 1), (x_side, 1), (y_side, 0), (across, 0), (across, 1)]
+    direct = len(arriving)
+    started = []
+
+    def start(*move):
+        item = copy(*move)
+        item.start()
+        started.append(item)
+
+    def begin():
+        for move in own:
+            start(*move)
+        for k in range(2):
+            start(me, k, direct + k, partner)
+
+    def receive(number):
+        block, k = arriving[number]
+        copy(block, k, number, partner).wait_recv()
+        if number in passed:
+            start(*passed[number])
+        start(block, k, direct + 2 + number, partner)
+
+    def finish():
+        for number in range(direct + 2):
+            copy(me, 0, direct + number, partner).wait_recv()
+
+    def drain():
+        for item in started:
+            item.wait_send()
+
+    return [x_side, y_side, partner], begin, receive, finish, drain
+
+
+def reduce_group(me, prefix, lasts, partial, boxes, sems, columns, packed, start):
+    each = boxes.shape[1]
+    cut = each // CUTS
+    row_tiles = each * packed
+    send, recv = sems
+    last = columns - 1
+    lane = lax.broadcasted_iota(jnp.int32, boxes.shape[2:], 1)
+    width = LANES // packed
+
+    def picked(dest, k):
+        values = [prefix[lasts[0, dest * row_tiles + h * each + k]] for h in range(packed)]
+        if packed == 1:
+            return values[0]
+        total = None
+        for turn in range(packed):
+            mixed = values[turn % packed]
+            for group in range(1, packed):
+                mixed = jnp.where(lane >= group * width, values[(group + turn) % packed], mixed)
+            mixed = pltpu.roll(mixed, turn * width, 1) if turn else mixed
+            total = mixed if total is None else total + mixed
+        return total
+
+    def each_tile(body):
+        def step(k, carry):
+            body(k)
+            return carry
+        return step
+
+    def copy(rightward, dest, piece):
+        part = pl.ds(piece * cut, cut)
+        place = dest - 1 if rightward else dest
+        number = ((0 if rightward else 1) * last + place) * CUTS + piece
+        here = dest - me if rightward else columns - me + dest
+        there = here - 1 if rightward else here + 1
+        ahead = 1 if rightward else -1
+        away = lambda: pltpu.make_async_remote_copy(
+            src_ref=boxes.at[here, part], dst_ref=boxes.at[there, part],
+            send_sem=send.at[number], recv_sem=recv.at[number],
+            device_id={"col": lax.axis_index("col") + ahead}, device_id_type=MESH)
+        home = lambda: pltpu.make_async_remote_copy(
+            src_ref=boxes.at[here, part], dst_ref=boxes.at[here, part],
+            send_sem=send.at[number], recv_sem=recv.at[number],
+            device_id={"col": lax.axis_index("col") + ahead}, device_id_type=MESH)
+        return here, away, home
+
+    sent = []
+
+    def open_chain(rightward, dest, piece):
+        here, away, _ = copy(rightward, dest, piece)
+
+        def body(k):
+            boxes[here, k] = picked(dest, k).astype(boxes.dtype)
+        lax.fori_loop(piece * cut, (piece + 1) * cut, each_tile(body), 0)
+        away().start()
+        sent.append(away)
+
+    def pass_on(rightward, dest, piece):
+        here, away, home = copy(rightward, dest, piece)
+        home().wait_recv()
+
+        def body(k):
+            boxes[here, k] = (partial[dest * each + k]
+                              + boxes[here, k].astype(jnp.float32)).astype(boxes.dtype)
+        lax.fori_loop(piece * cut, (piece + 1) * cut, each_tile(body), 0)
+        away().start()
+        sent.append(away)
+
+    def close_chain(rightward, piece):
+        here, _, home = copy(rightward, me, piece)
+        home().wait_recv()
+
+        def body(k):
+            partial[me * each + k] = partial[me * each + k] + boxes[here, k].astype(jnp.float32)
+        lax.fori_loop(piece * cut, (piece + 1) * cut, each_tile(body), 0)
+
+    def keep(dest):
+        def body(k):
+            partial[dest * each + k] = picked(dest, k)
+        lax.fori_loop(0, each, each_tile(body), 0)
+
+    def begin():
+        for turn in range(last):
+            for piece in range(CUTS):
+                if me == 0:
+                    open_chain(True, last - turn, piece)
+                if me == last:
+                    open_chain(False, turn, piece)
+        for dest in range(columns):
+            if dest == me or 0 < me < last:
+                keep(dest)
+
+    def arrival(rightward, dest, piece):
+        ahead = ((last - dest if rightward else dest) * CUTS + piece) * cut * TILE_TIME
+        hops = me if rightward else last - me
+        return start + ahead + hops * (cut * TILE_TIME + HOP_TIME)
+
+    events = []
+    for dest in range(columns):
+        for piece in range(CUTS):
+            for rightward in (True, False):
+                reached = (0 < me <= dest) if rightward else (dest <= me < last)
+                if not reached:
+                    continue
+                if dest == me:
+                    action = functools.partial(close_chain, rightward, piece)
+                else:
+                    action = functools.partial(pass_on, rightward, dest, piece)
+                events.append((arrival(rightward, dest, piece), dest == me, piece, action))
+
+    def drain():
+        for away in sent:
+            away().wait_send()
+
+    return begin, events, drain
+
+
+def layer_kernel(rows, columns, pairs, widths, features, tiles_hbm, tile_rows, tile_cols, valid,
+                 weight_hbm, bias_hbm, out, tiles, prefix, rows_v, cols_v, valid_v, codes_v, lasts_v,
+                 codes, lasts, weight, bias, own, masks, result, panels, partials, boxes, gather_sems,
+                 reduce_sems, local_sems, tile_sems, out_sems):
+    sub_tiles, tile_size, channels = features.shape
+    slot_count = tiles_hbm.shape[2]
+    groups = len(widths)
+    packs = [LANES // width for width in widths]
+    eaches = [sub_tiles // packed for packed in packs]
+    channel_of = [sum(widths[:g]) for g in range(groups)]
+    me_row, me_col = lax.axis_index("row"), lax.axis_index("col")
+    half = LANES // 2
+
+    def local(number, src, dst):
+        return pltpu.make_async_copy(src, dst, local_sems.at[number])
+
+    def own_block(g):
+        return pl.ds(me_row * eaches[g], eaches[g])
+
+    own_load = local(0, features.at[:, :, pl.ds(0, LANES)], own)
+    small = [local(1, tile_rows, rows_v), local(2, tile_cols, cols_v), local(3, valid, valid_v)]
+    whole = {g: local(6 + g, features.at[:, :, pl.ds(channel_of[g], LANES)], panels[g].at[own_block(g)])
+             for g in range(groups) if packs[g] == 1}
+    for item in [own_load] + small:
+        item.start()
+
+    gathers = [gather_group(panels[g], *gather_sems[g], eaches[g]) for g in range(groups)]
+    barrier = pltpu.get_barrier_semaphore()
+    peers = gathers[0][0]
+    for peer in peers:
+        pl.semaphore_signal(barrier, inc=1, device_id={"row": peer}, device_id_type=MESH)
+
+    @pl.when(me_col > 0)
+    def _():
+        pl.semaphore_signal(barrier, inc=1, device_id={"col": me_col - 1}, device_id_type=MESH)
+
+    @pl.when(me_col < columns - 1)
+    def _():
+        pl.semaphore_signal(barrier, inc=1, device_id={"col": me_col + 1}, device_id_type=MESH)
+
+    own_load.wait()
+    pack_own(own, panels[0], me_row * eaches[0], sub_tiles, widths[0], channel_of[0])
+
+    inside = jnp.logical_and(me_col > 0, me_col < columns - 1)
+
+    @pl.when(inside)
+    def _():
+        pl.semaphore_wait(barrier, len(peers) + 2)
+
+    @pl.when(jnp.logical_not(inside))
+    def _():
+        pl.semaphore_wait(barrier, len(peers) + 1)
+
+    gathers[0][1]()
+    share = slot_count // TILE_COPIES
+    loads = []
+    for k in range(TILE_COPIES):
+        part = pl.ds(k * share, share)
+        loads.append(pltpu.make_async_copy(
+            tiles_hbm.at[0, 0, part], tiles.at[part], tile_sems.at[k]))
+    params = [local(4, weight_hbm, weight), local(5, bias_hbm, bias)]
+    for item in loads + params + list(whole.values()):
+        item.start()
+    for item in small:
+        item.wait()
+    wanted_order(rows_v, cols_v, valid_v, codes_v, lasts_v, pairs)
+    lists = [local(1, codes_v, codes), local(2, lasts_v, lasts)]
+    for item in lists:
+        item.start()
+    for g in range(1, groups):
+        if packs[g] > 1:
+            pack_own(own, panels[g], me_row * eaches[g], sub_tiles, widths[g], channel_of[g])
+    lane = lax.broadcasted_iota(jnp.int32, masks.shape[1:], 1)
+    for h in range(2):
+        masks[h] = jnp.where(lax.shift_right_logical(lane, half.bit_length() - 1) == h,
+                             1.0, 0.0).astype(masks.dtype)
+    tiles[slot_count] = jnp.zeros(tiles.shape[1:], tiles.dtype)
+    prefix[pairs] = jnp.zeros(prefix.shape[1:], prefix.dtype)
+
+    here, links_free, starts, finishes = ENTRY_TIME + HOP_TIME, 0.0, [], []
+    for g in range(groups):
+        here += 3 * (eaches[g] // 2) * TILE_TIME
+        finishes.append(here + HOP_TIME)
+        ready = max(finishes[g], links_free if g == 0 else busy) + PRODUCT_TIME
+        busy = ready
+        starts.append(max(ready, links_free))
+        links_free = starts[g] + (columns - 1) * eaches[g] * TILE_TIME
+
+    def reduces_of(node):
+        return [reduce_group(node, prefix, lasts, partials[g], boxes[g], reduce_sems[g], columns,
+                             packs[g], starts[g]) for g in range(groups)]
+
+    reduces = [reduces_of(node) for node in range(columns)]
+    cut_rows = sub_tiles // CUTS * tile_size
+
+    def out_copy(piece):
+        part = pl.ds(piece * (sub_tiles // CUTS), sub_tiles // CUTS)
+        return pltpu.make_async_copy(result.at[part], out.at[part], out_sems.at[piece])
+
+    def mix(node, piece):
+        for tile in range(piece * (sub_tiles // CUTS), (piece + 1) * (sub_tiles // CUTS)):
+            mixed = bias[...]
+            for g in range(groups):
+                h, k = tile // eaches[g], tile % eaches[g]
+                summed = partials[g][node * eaches[g] + k].astype(jnp.bfloat16)
+                rows_of = weight[pl.ds(channel_of[g], widths[g]), :]
+                if packs[g] > 1:
+                    above = jnp.zeros((h * widths[g], channels), weight.dtype)
+                    below = jnp.zeros(((packs[g] - 1 - h) * widths[g], channels), weight.dtype)
+                    rows_of = jnp.concatenate(
+                        [part for part in (above, rows_of, below) if part.shape[0]], axis=0)
+                mixed = mixed + jnp.dot(summed, rows_of, preferred_element_type=jnp.float32)
+            result[tile] = mixed.astype(result.dtype)
+        out_copy(piece).start()
+
+    waiting = []
+    for node in range(columns):
+        events = [event for g in range(groups) for event in reduces[node][g][1]]
+        ends = {}
+        for when, closing, piece, _ in reduces[node][groups - 1][1]:
+            if closing:
+                ends[piece] = max(when, ends.get(piece, 0.0))
+        events += [(when, False, piece, functools.partial(mix, node, piece)) for piece, when in ends.items()]
+        waiting.append(sorted(events, key=lambda event: event[0]))
+
+    def serve(until):
+        for node in range(columns):
+            ready = [event for event in waiting[node] if event[0] <= until]
+            waiting[node] = [event for event in waiting[node] if event[0] > until]
+            if ready:
+                @pl.when(me_col == node)
+                def _():
+                    for event in ready:
+                        event[3]()
+
+    here = ENTRY_TIME + HOP_TIME
+    for g in range(groups):
+        _, _, receive, finish, _ = gathers[g]
+        for step in range(3):
+            here += eaches[g] // 2 * TILE_TIME
+            serve(here)
+            receive(2 * step)
+            receive(2 * step + 1)
+            if step == 0 and g + 1 < groups:
+                if g + 1 in whole:
+                    whole[g + 1].wait()
+                gathers[g + 1][1]()
+        serve(finishes[g])
+        finish()
+        if g == 0:
+            for item in lists + loads:
+                item.wait()
+        multiply(codes, tiles, panels[g], prefix, masks if packs[g] > 1 else None, pairs, sub_tiles)
+        for node in range(columns):
+            @pl.when(me_col == node)
+            def _():
+                reduces[node][g][0]()
+    for item in params:
+        item.wait()
+    serve(float("inf"))
+    for g in range(groups):
+        gathers[g][4]()
+    for node in range(columns):
+        @pl.when(me_col == node)
+        def _():
+            for g in range(groups):
+                reduces[node][g][2]()
+    for piece in range(CUTS):
+        out_copy(piece).wait()
+
+
+def layer(features, tiles, tile_rows, tile_cols, valid, weight, bias, rows, columns):
+    sub_rows, channels = features.shape
+    slot_count, tile_size = tiles.shape[2], tiles.shape[3]
+    widths = group_widths(channels)
+    sub_tiles = sub_rows // tile_size
+    row_tiles = sub_tiles * columns
+    pairs = -(-(slot_count // 2 + row_tiles) // (2 * PAIR_UNROLL)) * PAIR_UNROLL
+    codes_room = -(-2 * pairs // LANES) * LANES
+    vmem, smem, dma = pltpu.VMEM, pltpu.SMEM, pltpu.SemaphoreType.DMA
+    copies, moves = 14, 2 * (columns - 1) * CUTS
+    eaches = [sub_tiles * width // LANES for width in widths]
+    tile = (tile_size, LANES)
+    scratch = [
+        vmem((slot_count + 1, tile_size, tile_size), jnp.bfloat16),
+        vmem((pairs + 1,) + tile, jnp.float32),
+        vmem(tile_rows.shape, jnp.int32), vmem(tile_cols.shape, jnp.int32), vmem(valid.shape, jnp.int32),
+        vmem((1, codes_room), jnp.int32), vmem((1, LANES), jnp.int32),
+        smem((1, codes_room), jnp.int32), smem((1, LANES), jnp.int32),
+        vmem(weight.shape, weight.dtype), vmem((1, channels), bias.dtype),
+        vmem((sub_tiles,) + tile, jnp.bfloat16),
+        vmem((2,) + tile, jnp.bfloat16),
+        vmem((sub_tiles, tile_size, channels), jnp.bfloat16),
+        [vmem((rows * each,) + tile, jnp.bfloat16) for each in eaches],
+        [vmem((columns * each,) + tile, jnp.float32) for each in eaches],
+        [vmem((columns + 1, each) + tile, jnp.bfloat16) for each in eaches],
+        [[dma((copies,))] * 2 for _ in widths],
+        [[dma((moves,))] * 2 for _ in widths],
+        dma((len(widths) + 6,)), dma((TILE_COPIES,)), dma((CUTS,)),
+    ]
+    hbm = pl.BlockSpec(memory_space=pl.ANY)
+    mixed = pl.pallas_call(
+        functools.partial(layer_kernel, rows, columns, pairs, widths),
+        out_shape=jax.ShapeDtypeStruct((sub_tiles, tile_size, channels), jnp.bfloat16),
+        in_specs=[hbm] * 7, out_specs=hbm, scratch_shapes=scratch,
+        compiler_params=pltpu.CompilerParams(
+            collective_id=0, has_side_effects=True, vmem_limit_bytes=VMEM_ROOM),
+    )(features.reshape(sub_tiles, tile_size, channels), tiles, tile_rows, tile_cols, valid, weight,
+      bias.reshape(1, channels))
+    return jnp.maximum(mixed, 0).reshape(sub_rows, channels)
+
+
+def fits(features, tiles, rows, columns):
+    sub_rows, channels = features.shape
+    slot_count, tile_size = tiles.shape[2], tiles.shape[3]
+    sub_tiles = sub_rows // tile_size
+    if rows != 8 or channels % LANES or tile_size != LANES or slot_count % LANES or slot_count >= FIELD:
+        return False
+    if sub_tiles & (sub_tiles - 1) or sub_tiles < 2 * CUTS or columns < 2:
+        return False
+    row_tiles = sub_tiles * columns
+    tile_bytes = tile_size * tile_size * 2
+    pairs = (slot_count // 2 + row_tiles) // 2 + PAIR_UNROLL
+    held = slot_count + 2 * pairs + channels // LANES * (
+        sub_tiles * rows + 2 * row_tiles + sub_tiles * (columns + 2))
+    return row_tiles <= LANES and sub_tiles * rows <= FIELD and held * tile_bytes < VMEM_ROOM - 2**20
+
+
 def on_device(features, tiles, tile_rows, tile_cols, valid, weight, bias):
     sub_rows, channels = features.shape
     tile_size = tiles.shape[3]
     rows, columns = lax.axis_size("row"), lax.axis_size("col")
+    if fits(features, tiles, rows, columns):
+        return layer(features, tiles, tile_rows, tile_cols, valid, weight, bias, rows, columns)
     row_tiles = sub_rows * columns // tile_size
     width = min(channels, 128)
     lanes = channels // width

time: 161 us -> 107 us (0.66)
  Pallas kernels: 155 us -> 103 us
  other arithmetic: 0 us -> 2.26 us
  matrix products: 1.8 us -> 0 us
    pallas_call x5 -> x1, Pallas kernels: 155 us -> 103 us  [layer(): pl.pallas_call(functools.partial(layer_kernel, rows, columns, pairs, widt...]
    max x0 -> x1, other arithmetic: none -> 2.26 us  [layer(): return jnp.maximum(mixed, 0).reshape(sub_rows, channels)]
    dot_general x2 -> x0, matrix products: 1.8 us -> none  [on_device(): jnp.dot(sums[lane], weight[lane * width:(lane + 1) * width], preferred_el...]
where the time goes in v2:
time: 107 us; the launch traced here: 105 us
  Pallas kernels  103 us (96%)
  other arithmetic  2.26 us (2%)
    pallas_call x1, Pallas kernels, layer(): pl.pallas_call(functools.partial(layer_kernel, rows, columns, pairs, widt...  103 us
    max x1, other arithmetic, layer(): return jnp.maximum(mixed, 0).reshape(sub_rows, channels)  2.26 us

profile of v2, /device:TPU:18, one launch (start us, length us, event | category | flops | bytes accessed | tf_op | source)
XLA Modules:
  0.0 105.1 jit_solution(7507750383199331013)
XLA Ops:
  0.0 102.8 %shard_map.73 = bf16[16,128,256]{2,1,0:T(8,128)(2,1)} custom-call(bf16[16,128,256]{2,1,0:T(8,128)(2,1)} %bitcast.3, bf16[1,1,768,128,128]{4,3,2,1,0:T(8,128)(2,1)} %tiles_hbm.1, s32[1,1,768]{2,1,0:T(1,128)} %tile_rows.1, s32[1,1,768]{2,1,0:T(1,128)} %tile_cols.1, s32[1,1,768]{2,1,0:T(1,128)} %valid.1, bf16[256,256]{1,0:T(8,128)(2,1)} %weight_hbm.1, ...), custom_call_target="tpu_custom_call" | custom-call | tf_op jit(solution)/shard_map/pallas_call | solution.py:812
  102.8 2.3 %broadcast_maximum_fusion = bf16[16,128,256]{2,1,0:T(8,128)(2,1)} fusion(bf16[16,128,256]{2,1,0:T(8,128)(2,1)} %shard_map.73), kind=kLoop, calls=%fused_computation | loop fusion | flops 524288 | bytes 2097152 | tf_op jit(solution)/shard_map/max | solution.py:820

commit v3 on v2

--- a/solution.py
+++ b/solution.py
@@ -338,16 +338,17 @@
 FIELD_BITS = 10
 FIELD = 2**FIELD_BITS
 FIRST = FIELD * FIELD
-PAIR_UNROLL = 16
+PAIR_UNROLL = 28
 CUTS = 4
 TILE_COPIES = 8
 VMEM_ROOM = 63 * 2**20
-TILE_TIME, HOP_TIME, PRODUCT_TIME, ENTRY_TIME = 0.7, 1.8, 6.0, 3.0
+PRODUCT_PARTS = 4
+TILE_TIME, HOP_TIME, PRODUCT_TIME, PICK_TIME, ENTRY_TIME = 0.7, 1.8, 6.5, 1.5, 2.5
 
 
 def group_widths(channels):
-    half = LANES // 2
-    return (half, half) + (LANES,) * ((channels - LANES) // LANES)
+    first = (LANES // 4, LANES // 4, LANES // 2)
+    return first + (LANES,) * ((channels - LANES) // LANES)
 
 
 def wanted_order(rows_v, cols_v, valid_v, codes_v, lasts_v, pairs):
@@ -408,8 +409,7 @@
     lax.fori_loop(0, each, body, 0)
 
 
-def multiply(codes, tiles, panel, prefix, masks, pairs, sub_tiles):
-    packed = masks.shape[0] if masks is not None else 1
+def multiply(codes, tiles, panel, prefix, masks, first, last, total, packed, sub_tiles):
     each = sub_tiles // packed
 
     def operands(code):
@@ -422,7 +422,9 @@
         block = lax.shift_right_logical(upper, packed.bit_length() - 1)
         share = jnp.bitwise_and(upper, packed - 1)
         value = panel[block * each + jnp.bitwise_and(column, each - 1)]
-        return tile, value * masks[share]
+        lane = lax.broadcasted_iota(jnp.int32, value.shape, 1)
+        kept = lax.shift_right_logical(lane, (LANES // packed).bit_length() - 1) == share
+        return tile, jnp.where(kept, value, 0)
 
     def body(step, total):
         for k in range(PAIR_UNROLL):
@@ -438,7 +440,7 @@
             prefix[pair] = total
         return total
 
-    lax.fori_loop(0, pairs // PAIR_UNROLL, body, jnp.zeros(panel.shape[1:], jnp.float32))
+    return lax.fori_loop(first, last, body, total)
 
 
 def gather_group(panel, send_sem, recv_sem, each):
@@ -492,7 +494,7 @@
     return [x_side, y_side, partner], begin, receive, finish, drain
 
 
-def reduce_group(me, prefix, lasts, partial, boxes, sems, columns, packed, start):
+def reduce_group(me, prefix, lasts, partial, boxes, sems, columns, packed):
     each = boxes.shape[1]
     cut = each // CUTS
     row_tiles = each * packed
@@ -542,9 +544,8 @@
     def open_chain(rightward, dest, piece):
         here, away, _ = copy(rightward, dest, piece)
 
-        def body(k):
+        for k in range(piece * cut, (piece + 1) * cut):
             boxes[here, k] = picked(dest, k).astype(boxes.dtype)
-        lax.fori_loop(piece * cut, (piece + 1) * cut, each_tile(body), 0)
         away().start()
         sent.append(away)
 
@@ -586,7 +587,7 @@
     def arrival(rightward, dest, piece):
         ahead = ((last - dest if rightward else dest) * CUTS + piece) * cut * TILE_TIME
         hops = me if rightward else last - me
-        return start + ahead + hops * (cut * TILE_TIME + HOP_TIME)
+        return ahead + hops * (cut * TILE_TIME + HOP_TIME)
 
     events = []
     for dest in range(columns):
@@ -619,7 +620,7 @@
     eaches = [sub_tiles // packed for packed in packs]
     channel_of = [sum(widths[:g]) for g in range(groups)]
     me_row, me_col = lax.axis_index("row"), lax.axis_index("col")
-    half = LANES // 2
+    masks = dict(zip(sorted(set(packs) - {1}), masks))
 
     def local(number, src, dst):
         return pltpu.make_async_copy(src, dst, local_sems.at[number])
@@ -680,35 +681,23 @@
     for g in range(1, groups):
         if packs[g] > 1:
             pack_own(own, panels[g], me_row * eaches[g], sub_tiles, widths[g], channel_of[g])
-    lane = lax.broadcasted_iota(jnp.int32, masks.shape[1:], 1)
-    for h in range(2):
-        masks[h] = jnp.where(lax.shift_right_logical(lane, half.bit_length() - 1) == h,
-                             1.0, 0.0).astype(masks.dtype)
+    lane = lax.broadcasted_iota(jnp.int32, tiles.shape[1:], 1)
+    for packed, mask in masks.items():
+        for h in range(packed):
+            inside_h = jnp.logical_and(lane >= h * (LANES // packed), lane < (h + 1) * (LANES // packed))
+            mask[h] = jnp.where(inside_h, 1.0, 0.0).astype(mask.dtype)
     tiles[slot_count] = jnp.zeros(tiles.shape[1:], tiles.dtype)
     prefix[pairs] = jnp.zeros(prefix.shape[1:], prefix.dtype)
 
-    here, links_free, starts, finishes = ENTRY_TIME + HOP_TIME, 0.0, [], []
-    for g in range(groups):
-        here += 3 * (eaches[g] // 2) * TILE_TIME
-        finishes.append(here + HOP_TIME)
-        ready = max(finishes[g], links_free if g == 0 else busy) + PRODUCT_TIME
-        busy = ready
-        starts.append(max(ready, links_free))
-        links_free = starts[g] + (columns - 1) * eaches[g] * TILE_TIME
-
-    def reduces_of(node):
-        return [reduce_group(node, prefix, lasts, partials[g], boxes[g], reduce_sems[g], columns,
-                             packs[g], starts[g]) for g in range(groups)]
-
-    reduces = [reduces_of(node) for node in range(columns)]
-    cut_rows = sub_tiles // CUTS * tile_size
+    reduces = [[reduce_group(node, prefix, lasts, partials[g], boxes[g], reduce_sems[g], columns, packs[g])
+                for g in range(groups)] for node in range(columns)]
 
     def out_copy(piece):
         part = pl.ds(piece * (sub_tiles // CUTS), sub_tiles // CUTS)
         return pltpu.make_async_copy(result.at[part], out.at[part], out_sems.at[piece])
 
     def mix(node, piece):
-        for tile in range(piece * (sub_tiles // CUTS), (piece + 1) * (sub_tiles // CUTS)):
+        for tile in range(piece * sub_tiles // CUTS, (piece + 1) * sub_tiles // CUTS):
             mixed = bias[...]
             for g in range(groups):
                 h, k = tile // eaches[g], tile % eaches[g]
@@ -723,15 +712,21 @@
             result[tile] = mixed.astype(result.dtype)
         out_copy(piece).start()
 
-    waiting = []
-    for node in range(columns):
-        events = [event for g in range(groups) for event in reduces[node][g][1]]
-        ends = {}
-        for when, closing, piece, _ in reduces[node][groups - 1][1]:
-            if closing:
-                ends[piece] = max(when, ends.get(piece, 0.0))
-        events += [(when, False, piece, functools.partial(mix, node, piece)) for piece, when in ends.items()]
-        waiting.append(sorted(events, key=lambda event: event[0]))
+    waiting, later = [[] for _ in range(columns)], [[] for _ in range(columns)]
+
+    def expect(g, start):
+        for node in range(columns):
+            events = [(start + when, action) for when, closing, _, action in reduces[node][g][1]
+                      if g == groups - 1 or not closing]
+            later[node] += [(start + when, action) for when, closing, _, action in reduces[node][g][1]
+                            if g < groups - 1 and closing]
+            if g == groups - 1:
+                events += [(max(when, start), action) for when, action in later[node]]
+                for piece in range(CUTS):
+                    when = max(when for when, closing, part, _ in reduces[node][g][1]
+                               if closing and part == piece)
+                    events.append((start + when + 0.01, functools.partial(mix, node, piece)))
+            waiting[node] = sorted(waiting[node] + events, key=lambda event: event[0])
 
     def serve(until):
         for node in range(columns):
@@ -741,30 +736,68 @@
                 @pl.when(me_col == node)
                 def _():
                     for event in ready:
-                        event[3]()
-
-    here = ENTRY_TIME + HOP_TIME
+                        event[1]()
+
+    now = ENTRY_TIME
+    wires, sends = now, now
+    arrivals, finals = [], {}
+
+    def begin_gather(g):
+        nonlocal wires
+        if g in whole:
+            whole[g].wait()
+        gathers[g][1]()
+        cut_time = eaches[g] // 2 * TILE_TIME
+        wires = max(wires, now)
+        arrivals.extend([(wires + cut_time + HOP_TIME, g, 0), (wires + 2 * cut_time + HOP_TIME, g, 1)])
+        wires += 2 * cut_time
+
+    def take_arrival():
+        nonlocal wires
+        arrivals.sort()
+        _, g, step = arrivals.pop(0)
+        if step < 3:
+            gathers[g][2](2 * step)
+            gathers[g][2](2 * step + 1)
+        if step == 0:
+            cut_time = eaches[g] // 2 * TILE_TIME
+            wires = max(wires, now) + cut_time
+            arrivals.append((wires + HOP_TIME, g, 2))
+            if g + 1 < groups:
+                begin_gather(g + 1)
+        if step == 2:
+            arrivals.append((now + HOP_TIME, g, 3))
+        if step == 3:
+            gathers[g][3]()
+
+    arrivals = [(now + (k + 1) * (eaches[0] // 2) * TILE_TIME + HOP_TIME, 0, k) for k in range(2)]
+    wires += eaches[0] // 2 * TILE_TIME * 2
+    finished = 0
     for g in range(groups):
-        _, _, receive, finish, _ = gathers[g]
-        for step in range(3):
-            here += eaches[g] // 2 * TILE_TIME
-            serve(here)
-            receive(2 * step)
-            receive(2 * step + 1)
-            if step == 0 and g + 1 < groups:
-                if g + 1 in whole:
-                    whole[g + 1].wait()
-                gathers[g + 1][1]()
-        serve(finishes[g])
-        finish()
-        if g == 0:
-            for item in lists + loads:
-                item.wait()
-        multiply(codes, tiles, panels[g], prefix, masks if packs[g] > 1 else None, pairs, sub_tiles)
+        for part in range(PRODUCT_PARTS):
+            while arrivals and (min(arrivals)[0] <= now or finished <= g):
+                now = max(now, min(arrivals)[0])
+                serve(now)
+                finished += min(arrivals)[2] == 3
+                take_arrival()
+            serve(now)
+            if g == 0 and part == 0:
+                for item in lists + loads:
+                    item.wait()
+            steps = pairs // PAIR_UNROLL
+            total = jnp.zeros(panels[g].shape[1:], jnp.float32) if part == 0 else total
+            total = multiply(codes, tiles, panels[g], prefix, masks.get(packs[g]),
+                             part * steps // PRODUCT_PARTS, (part + 1) * steps // PRODUCT_PARTS,
+                             total, packs[g], sub_tiles)
+            now += PRODUCT_TIME / PRODUCT_PARTS
         for node in range(columns):
             @pl.when(me_col == node)
             def _():
                 reduces[node][g][0]()
+        sends = max(sends, now)
+        expect(g, sends)
+        sends += (columns - 1) * eaches[g] * TILE_TIME
+        now += PICK_TIME
     for item in params:
         item.wait()
     serve(float("inf"))
@@ -790,6 +823,7 @@
     vmem, smem, dma = pltpu.VMEM, pltpu.SMEM, pltpu.SemaphoreType.DMA
     copies, moves = 14, 2 * (columns - 1) * CUTS
     eaches = [sub_tiles * width // LANES for width in widths]
+    packs = sorted({LANES // width for width in widths} - {1})
     tile = (tile_size, LANES)
     scratch = [
         vmem((slot_count + 1, tile_size, tile_size), jnp.bfloat16),
@@ -799,7 +833,7 @@
         smem((1, codes_room), jnp.int32), smem((1, LANES), jnp.int32),
         vmem(weight.shape, weight.dtype), vmem((1, channels), bias.dtype),
         vmem((sub_tiles,) + tile, jnp.bfloat16),
-        vmem((2,) + tile, jnp.bfloat16),
+        [vmem((packed,) + tile, jnp.bfloat16) for packed in packs],
         vmem((sub_tiles, tile_size, channels), jnp.bfloat16),
         [vmem((rows * each,) + tile, jnp.bfloat16) for each in eaches],
         [vmem((columns * each,) + tile, jnp.float32) for each in eaches],
@@ -826,7 +860,7 @@
     sub_tiles = sub_rows // tile_size
     if rows != 8 or channels % LANES or tile_size != LANES or slot_count % LANES or slot_count >= FIELD:
         return False
-    if sub_tiles & (sub_tiles - 1) or sub_tiles < 2 * CUTS or columns < 2:
+    if sub_tiles & (sub_tiles - 1) or sub_tiles < 4 * CUTS or columns < 2:
         return False
     row_tiles = sub_tiles * columns
     tile_bytes = tile_size * tile_size * 2

time: 107 us -> 93 us (0.87); the launches traced: 105 us -> 92.5 us
  Pallas kernels: 103 us -> 90.2 us
    pallas_call x1, Pallas kernels: 103 us -> 90.2 us  [layer(): pl.pallas_call(functools.partial(layer_kernel, rows, columns, pairs, widt...]
where the time goes in v3:
time: 93 us; the launch traced here: 92.5 us
  Pallas kernels  90.2 us (97%)
  other arithmetic  2.26 us (2%)
    pallas_call x1, Pallas kernels, layer(): pl.pallas_call(functools.partial(layer_kernel, rows, columns, pairs, widt...  90.2 us
    max x1, other arithmetic, layer(): return jnp.maximum(mixed, 0).reshape(sub_rows, channels)  2.26 us

profile of v3, /device:TPU:18, one launch (start us, length us, event | category | flops | bytes accessed | tf_op | source)
XLA Modules:
  0.0 92.5 jit_solution(10430343236556412669)
XLA Ops:
  0.0 90.2 %shard_map.73 = bf16[16,128,256]{2,1,0:T(8,128)(2,1)} custom-call(bf16[16,128,256]{2,1,0:T(8,128)(2,1)} %bitcast.3, bf16[1,1,768,128,128]{4,3,2,1,0:T(8,128)(2,1)} %tiles_hbm.1, s32[1,1,768]{2,1,0:T(1,128)} %tile_rows.1, s32[1,1,768]{2,1,0:T(1,128)} %tile_cols.1, s32[1,1,768]{2,1,0:T(1,128)} %valid.1, bf16[256,256]{1,0:T(8,128)(2,1)} %weight_hbm.1, ...), custom_call_target="tpu_custom_call" | custom-call | tf_op jit(solution)/shard_map/pallas_call | solution.py:846
  90.2 2.3 %broadcast_maximum_fusion = bf16[16,128,256]{2,1,0:T(8,128)(2,1)} fusion(bf16[16,128,256]{2,1,0:T(8,128)(2,1)} %shard_map.73), kind=kLoop, calls=%fused_computation | loop fusion | flops 524288 | bytes 2097152 | tf_op jit(solution)/shard_map/max | solution.py:854

commit v4 on v3

--- a/solution.py
+++ b/solution.py
@@ -338,12 +338,12 @@
 FIELD_BITS = 10
 FIELD = 2**FIELD_BITS
 FIRST = FIELD * FIELD
-PAIR_UNROLL = 28
+PAIR_UNROLL = 56
 CUTS = 4
 TILE_COPIES = 8
-VMEM_ROOM = 63 * 2**20
-PRODUCT_PARTS = 4
-TILE_TIME, HOP_TIME, PRODUCT_TIME, PICK_TIME, ENTRY_TIME = 0.7, 1.8, 6.5, 1.5, 2.5
+VMEM_ROOM = 62 * 2**20
+PRODUCT_PARTS = 2
+TILE_TIME, HOP_TIME, PRODUCT_TIME, PICK_TIME, ENTRY_TIME, LANDING_TIME, LATER_TIME = 0.7, 1.8, 5.0, 2.5, 1.6, 3.0, 0.6
 
 
 def group_widths(channels):
@@ -409,7 +409,7 @@
     lax.fori_loop(0, each, body, 0)
 
 
-def multiply(codes, tiles, panel, prefix, masks, first, last, total, packed, sub_tiles):
+def multiply(codes, tiles, panel, prefix, first, last, total, packed, sub_tiles):
     each = sub_tiles // packed
 
     def operands(code):
@@ -611,8 +611,8 @@
 
 def layer_kernel(rows, columns, pairs, widths, features, tiles_hbm, tile_rows, tile_cols, valid,
                  weight_hbm, bias_hbm, out, tiles, prefix, rows_v, cols_v, valid_v, codes_v, lasts_v,
-                 codes, lasts, weight, bias, own, masks, result, panels, partials, boxes, gather_sems,
-                 reduce_sems, local_sems, tile_sems, out_sems):
+                 codes, lasts, weight, bias, own, panels, partials, boxes, gather_sems,
+                 reduce_sems, local_sems, tile_sems):
     sub_tiles, tile_size, channels = features.shape
     slot_count = tiles_hbm.shape[2]
     groups = len(widths)
@@ -620,7 +620,6 @@
     eaches = [sub_tiles // packed for packed in packs]
     channel_of = [sum(widths[:g]) for g in range(groups)]
     me_row, me_col = lax.axis_index("row"), lax.axis_index("col")
-    masks = dict(zip(sorted(set(packs) - {1}), masks))
 
     def local(number, src, dst):
         return pltpu.make_async_copy(src, dst, local_sems.at[number])
@@ -681,20 +680,11 @@
     for g in range(1, groups):
         if packs[g] > 1:
             pack_own(own, panels[g], me_row * eaches[g], sub_tiles, widths[g], channel_of[g])
-    lane = lax.broadcasted_iota(jnp.int32, tiles.shape[1:], 1)
-    for packed, mask in masks.items():
-        for h in range(packed):
-            inside_h = jnp.logical_and(lane >= h * (LANES // packed), lane < (h + 1) * (LANES // packed))
-            mask[h] = jnp.where(inside_h, 1.0, 0.0).astype(mask.dtype)
     tiles[slot_count] = jnp.zeros(tiles.shape[1:], tiles.dtype)
     prefix[pairs] = jnp.zeros(prefix.shape[1:], prefix.dtype)
 
     reduces = [[reduce_group(node, prefix, lasts, partials[g], boxes[g], reduce_sems[g], columns, packs[g])
                 for g in range(groups)] for node in range(columns)]
-
-    def out_copy(piece):
-        part = pl.ds(piece * (sub_tiles // CUTS), sub_tiles // CUTS)
-        return pltpu.make_async_copy(result.at[part], out.at[part], out_sems.at[piece])
 
     def mix(node, piece):
         for tile in range(piece * sub_tiles // CUTS, (piece + 1) * sub_tiles // CUTS):
@@ -709,8 +699,7 @@
                     rows_of = jnp.concatenate(
                         [part for part in (above, rows_of, below) if part.shape[0]], axis=0)
                 mixed = mixed + jnp.dot(summed, rows_of, preferred_element_type=jnp.float32)
-            result[tile] = mixed.astype(result.dtype)
-        out_copy(piece).start()
+            out[tile] = mixed.astype(out.dtype)
 
     waiting, later = [[] for _ in range(columns)], [[] for _ in range(columns)]
 
@@ -749,7 +738,8 @@
         gathers[g][1]()
         cut_time = eaches[g] // 2 * TILE_TIME
         wires = max(wires, now)
-        arrivals.extend([(wires + cut_time + HOP_TIME, g, 0), (wires + 2 * cut_time + HOP_TIME, g, 1)])
+        landing = LANDING_TIME + LATER_TIME * g
+        arrivals.extend([(wires + cut_time + landing, g, 0), (wires + 2 * cut_time + landing, g, 1)])
         wires += 2 * cut_time
 
     def take_arrival():
@@ -762,7 +752,7 @@
         if step == 0:
             cut_time = eaches[g] // 2 * TILE_TIME
             wires = max(wires, now) + cut_time
-            arrivals.append((wires + HOP_TIME, g, 2))
+            arrivals.append((wires + LANDING_TIME, g, 2))
             if g + 1 < groups:
                 begin_gather(g + 1)
         if step == 2:
@@ -770,7 +760,7 @@
         if step == 3:
             gathers[g][3]()
 
-    arrivals = [(now + (k + 1) * (eaches[0] // 2) * TILE_TIME + HOP_TIME, 0, k) for k in range(2)]
+    arrivals = [(now + (k + 1) * (eaches[0] // 2) * TILE_TIME + LANDING_TIME, 0, k) for k in range(2)]
     wires += eaches[0] // 2 * TILE_TIME * 2
     finished = 0
     for g in range(groups):
@@ -786,10 +776,13 @@
                     item.wait()
             steps = pairs // PAIR_UNROLL
             total = jnp.zeros(panels[g].shape[1:], jnp.float32) if part == 0 else total
-            total = multiply(codes, tiles, panels[g], prefix, masks.get(packs[g]),
+            total = multiply(codes, tiles, panels[g], prefix,
                              part * steps // PRODUCT_PARTS, (part + 1) * steps // PRODUCT_PARTS,
                              total, packs[g], sub_tiles)
             now += PRODUCT_TIME / PRODUCT_PARTS
+        while arrivals and min(arrivals)[0] <= now:
+            finished += min(arrivals)[2] == 3
+            take_arrival()
         for node in range(columns):
             @pl.when(me_col == node)
             def _():
@@ -808,8 +801,10 @@
         def _():
             for g in range(groups):
                 reduces[node][g][2]()
-    for piece in range(CUTS):
-        out_copy(piece).wait()
+
+
+def pair_count(slot_count, row_tiles):
+    return -(-(slot_count // 2 + row_tiles) // (2 * PAIR_UNROLL)) * PAIR_UNROLL
 
 
 def layer(features, tiles, tile_rows, tile_cols, valid, weight, bias, rows, columns):
@@ -818,12 +813,11 @@
     widths = group_widths(channels)
     sub_tiles = sub_rows // tile_size
     row_tiles = sub_tiles * columns
-    pairs = -(-(slot_count // 2 + row_tiles) // (2 * PAIR_UNROLL)) * PAIR_UNROLL
+    pairs = pair_count(slot_count, row_tiles)
     codes_room = -(-2 * pairs // LANES) * LANES
     vmem, smem, dma = pltpu.VMEM, pltpu.SMEM, pltpu.SemaphoreType.DMA
     copies, moves = 14, 2 * (columns - 1) * CUTS
     eaches = [sub_tiles * width // LANES for width in widths]
-    packs = sorted({LANES // width for width in widths} - {1})
     tile = (tile_size, LANES)
     scratch = [
         vmem((slot_count + 1, tile_size, tile_size), jnp.bfloat16),
@@ -833,20 +827,18 @@
         smem((1, codes_room), jnp.int32), smem((1, LANES), jnp.int32),
         vmem(weight.shape, weight.dtype), vmem((1, channels), bias.dtype),
         vmem((sub_tiles,) + tile, jnp.bfloat16),
-        [vmem((packed,) + tile, jnp.bfloat16) for packed in packs],
-        vmem((sub_tiles, tile_size, channels), jnp.bfloat16),
         [vmem((rows * each,) + tile, jnp.bfloat16) for each in eaches],
         [vmem((columns * each,) + tile, jnp.float32) for each in eaches],
         [vmem((columns + 1, each) + tile, jnp.bfloat16) for each in eaches],
         [[dma((copies,))] * 2 for _ in widths],
         [[dma((moves,))] * 2 for _ in widths],
-        dma((len(widths) + 6,)), dma((TILE_COPIES,)), dma((CUTS,)),
+        dma((len(widths) + 6,)), dma((TILE_COPIES,)),
     ]
     hbm = pl.BlockSpec(memory_space=pl.ANY)
     mixed = pl.pallas_call(
         functools.partial(layer_kernel, rows, columns, pairs, widths),
-        out_shape=jax.ShapeDtypeStruct((sub_tiles, tile_size, channels), jnp.bfloat16),
-        in_specs=[hbm] * 7, out_specs=hbm, scratch_shapes=scratch,
+        out_shape=pltpu.VMEM((sub_tiles, tile_size, channels), jnp.bfloat16),
+        in_specs=[hbm] * 7, out_specs=pl.BlockSpec(memory_space=pltpu.VMEM), scratch_shapes=scratch,
         compiler_params=pltpu.CompilerParams(
             collective_id=0, has_side_effects=True, vmem_limit_bytes=VMEM_ROOM),
     )(features.reshape(sub_tiles, tile_size, channels), tiles, tile_rows, tile_cols, valid, weight,
@@ -864,10 +856,10 @@
         return False
     row_tiles = sub_tiles * columns
     tile_bytes = tile_size * tile_size * 2
-    pairs = (slot_count // 2 + row_tiles) // 2 + PAIR_UNROLL
+    pairs = pair_count(slot_count, row_tiles)
     held = slot_count + 2 * pairs + channels // LANES * (
         sub_tiles * rows + 2 * row_tiles + sub_tiles * (columns + 2))
-    return row_tiles <= LANES and sub_tiles * rows <= FIELD and held * tile_bytes < VMEM_ROOM - 2**20
+    return row_tiles <= LANES and sub_tiles * rows <= FIELD and held * tile_bytes < VMEM_ROOM
 
 
 def on_device(features, tiles, tile_rows, tile_cols, valid, weight, bias):

time: 93 us -> 90.8 us (0.976)
  other arithmetic: 2.26 us -> 1.04 us
    max x1, other arithmetic: 2.26 us -> 1.04 us  [layer(): return jnp.maximum(mixed, 0).reshape(sub_rows, channels)]
where the time goes in v4:
time: 90.8 us; the launch traced here: 90.3 us
  Pallas kernels  89.3 us (98%)
  other arithmetic  1.04 us (1%)
    pallas_call x1, Pallas kernels, layer(): pl.pallas_call(functools.partial(layer_kernel, rows, columns, pairs, widt...  89.3 us

profile of v4, /device:TPU:18, one launch (start us, length us, event | category | flops | bytes accessed | tf_op | source)
XLA Modules:
  0.0 90.3 jit_solution(9363050797188175723)
XLA Ops:
  0.0 89.3 %shard_map.73 = bf16[16,128,256]{2,1,0:T(8,128)(2,1)S(1)} custom-call(bf16[16,128,256]{2,1,0:T(8,128)(2,1)} %bitcast.3, bf16[1,1,768,128,128]{4,3,2,1,0:T(8,128)(2,1)} %tiles_hbm.1, s32[1,1,768]{2,1,0:T(1,128)} %tile_rows.1, s32[1,1,768]{2,1,0:T(1,128)} %tile_cols.1, s32[1,1,768]{2,1,0:T(1,128)} %valid.1, bf16[256,256]{1,0:T(8,128)(2,1)} %weight_hbm.1, ...), custom_call_target="tpu_custom_call" | custom-call | tf_op jit(solution)/shard_map/pallas_call | solution.py:838
  89.3 1.0 %broadcast_maximum_fusion = bf16[16,128,256]{2,1,0:T(8,128)(2,1)} fusion(bf16[16,128,256]{2,1,0:T(8,128)(2,1)S(1)} %shard_map.73), kind=kLoop, calls=%fused_computation | loop fusion | flops 524288 | bytes 2097152 | tf_op jit(solution)/shard_map/max | solution.py:846
